TPU v7x, 32 devices: a whole 2x2x4 slice. The times are simulated.
32 devices in a mesh: bead: 8 (over z, core), atom: 4 (over y, x).
Axes of the slice: x: 2, y: 2, z: 4, core: 2. Of those that a mesh axis runs over, the one named last changes fastest.
Arguments:
- positions: float32 [32, 3, 4096], P('bead', None, 'atom'), may hold values from -6 to 6
- momenta: float32 [32, 3, 4096], P('bead', None, 'atom'), may hold values from -6 to 6
- charge: float32 [4096], P('atom'), may hold values from -1 to 1
- masses: float32 [4096], P('atom'), may hold values from 0.5 to 4
- pair_local: int32 [128], P('atom'), may hold values from 0 to 31, as said below
- pair_other: int32 [128], P('atom'), may hold values from 0 to 31, as said below
- pair_count: int32 [4], P('atom'), may hold values from 0 to 32, as said below
Outputs:
- new_positions: float32 [32, 3, 4096], P('bead', None, 'atom')
- new_momenta: float32 [32, 3, 4096], P('bead', None, 'atom')
- spring: float32 [4096], P('atom')
Inputs may be any that keep to these rules, and one draw needn't show every extreme that they name: `pair_local`: the slots of atom block d (slots d * 32 to (d + 1) * 32 - 1) name tiles of that block: d * 8 to (d + 1) * 8 - 1. `pair_other`: each slot's neighbour tile lies within 8 tiles of its tile, counting cyclically over 32 tiles. `pair_count`: the counts of blocks d and d + 2 sum to at most 32.
All inputs are finite; a program needn't handle non-finite values.
Results may differ from a plain program's by a relative error of at most 0.000071.
Values sent between devices are 32-bit elements; how exact they have to be, the bound alone decides.
A program may use at most 64 MiB of HBM per device.

v0:
```python
import jax
import jax.numpy as jnp
from jax import lax
from jax.sharding import PartitionSpec as P

time_step = 1.0
omega_cycle = 1.2
width_sq = 2.0


def extended(block, sides, width):
    for axis, dim in sides:
        count = lax.axis_size(axis)
        forward = [(i, i + 1) for i in range(count - 1)]
        forward.append((count - 1, 0))
        backward = [(target, source) for source, target in forward]
        low = lax.ppermute(
            lax.slice_in_dim(block, block.shape[dim] - width, None, axis=dim), axis, forward
        )
        high = lax.ppermute(lax.slice_in_dim(block, 0, width, axis=dim), axis, backward)
        block = jnp.concatenate([low, block, high], axis=dim)
    return block


def cycle_table(beads):
    bead_index = jnp.arange(beads, dtype=jnp.float32)[:, None]
    mode_index = jnp.arange(beads, dtype=jnp.float32)[None, :]
    middle = beads // 2
    angle = 2.0 * jnp.pi * bead_index * mode_index / beads
    cosine_part = jnp.sqrt(2.0 / beads) * jnp.cos(angle)
    sine_part = jnp.sqrt(2.0 / beads) * jnp.sin(angle)
    edge_part = jnp.sqrt(1.0 / beads) * jnp.cos(jnp.pi * bead_index)
    first = jnp.sqrt(1.0 / beads) * jnp.ones_like(angle)
    table = jnp.where(
        mode_index == 0,
        first,
        jnp.where(
            mode_index < middle, cosine_part, jnp.where(mode_index == middle, edge_part, sine_part)
        ),
    )
    frequency = 2.0 * omega_cycle * jnp.sin(jnp.pi * jnp.arange(beads, dtype=jnp.float32) / beads)
    return (table, frequency)


def pair_force(left_pos, right_pos, left_charge, right_charge):
    separation = left_pos[..., :, None] - right_pos[..., None, :]
    dist_sq = jnp.sum(separation * separation, axis=-3)
    weights = (
        left_charge[..., :, None]
        * right_charge[..., None, :]
        * jnp.exp(-dist_sq / (2.0 * width_sq))
        / width_sq
    )
    return jnp.sum(separation * weights[..., None, :, :], axis=-1)


def propagate(mode_pos, mode_mom, frequency, masses, beads):
    freq_col = frequency[:, None, None]
    mass_row = masses[None, None, :]
    cosine = jnp.cos(freq_col * time_step)
    sine = jnp.sin(freq_col * time_step)
    reach = jnp.where(freq_col > 0, sine / jnp.where(freq_col > 0, freq_col, 1.0), time_step)
    moved_pos = cosine * mode_pos + reach * mode_mom / mass_row
    moved_mom = -mass_row * freq_col * sine * mode_pos + cosine * mode_mom
    spring = (
        jnp.sum(0.5 * mass_row * freq_col * freq_col * moved_pos * moved_pos, axis=(0, 1)) / beads
    )
    return (moved_pos, moved_mom, spring)


def slot_forces(packed):
    slots = packed.shape[0]
    blocks = packed.reshape((slots // 4, 4) + packed.shape[1:])

    def one_block(block_pack):
        return pair_force(
            block_pack[:, 0, :, :3],
            block_pack[:, 1, :, :3],
            block_pack[:, 0, :, 3],
            block_pack[:, 1, :, 3],
        )

    result = lax.map(one_block, blocks)
    return result.reshape((slots,) + result.shape[2:])


def on_device(positions, momenta, charge, masses, pair_local, pair_other, pair_count):
    bead_dev, _, atom_dev = positions.shape
    tile_atoms = 128
    tile_dev = atom_dev // tile_atoms
    atom_count = lax.axis_size("atom")
    bead_count = lax.axis_size("bead")
    beads = bead_dev * bead_count
    tiles = tile_dev * atom_count
    slots = pair_local.shape[0]
    hp = lax.Precision.HIGHEST
    table, frequency = cycle_table(beads)
    sub_atoms = atom_dev // bead_count
    gathered_pos = lax.all_to_all(positions, "bead", split_axis=2, concat_axis=0, tiled=True)
    charge_rows = jnp.broadcast_to(charge[None, None, :], (bead_dev, 1, atom_dev))
    packed = jnp.concatenate([positions, charge_rows], axis=1)
    haloed = extended(packed, (("atom", 2),), atom_dev)
    ext_tiles = jnp.transpose(haloed.reshape(bead_dev, 4, 3 * tile_dev, tile_atoms), (2, 0, 1, 3))
    base_tile = lax.axis_index("atom") * tile_dev - tile_dev
    left_local = (pair_local - base_tile) % tiles
    right_local = (pair_other - base_tile) % tiles
    live_count = pair_count[0]
    slot_ids = jnp.arange(slots)
    live_mask = (slot_ids < live_count).astype(jnp.float32)
    left_block = jnp.take(ext_tiles, left_local, axis=0)
    right_block = jnp.take(ext_tiles, right_local, axis=0)
    left_block = jnp.concatenate(
        [left_block[:, :, :3], left_block[:, :, 3:] * live_mask[:, None, None, None]], axis=2
    )
    forces = slot_forces(jnp.stack([left_block, right_block], axis=1))
    onehot = (left_local[None, :] - tile_dev == jnp.arange(tile_dev)[:, None]).astype(jnp.float32)
    summed = jnp.einsum("ts,sbca->bcta", onehot, forces, precision=hp)
    force = summed.reshape(bead_dev, 3, atom_dev)
    kicked = momenta + 0.5 * time_step * force
    gathered_mom = lax.all_to_all(kicked, "bead", split_axis=2, concat_axis=0, tiled=True)
    mode_pos = jnp.einsum("jk,jca->kca", table, gathered_pos, precision=hp)
    mode_mom = jnp.einsum("jk,jca->kca", table, gathered_mom, precision=hp)
    sub_masses = lax.dynamic_slice_in_dim(masses, lax.axis_index("bead") * sub_atoms, sub_atoms, 0)
    moved_pos, moved_mom, spring_sub = propagate(mode_pos, mode_mom, frequency, sub_masses, beads)
    stacked = jnp.stack([moved_pos, moved_mom], axis=1)
    returned_rows = jnp.einsum("jk,kxca->jxca", table, stacked, precision=hp)
    result = lax.all_to_all(returned_rows, "bead", split_axis=0, concat_axis=3, tiled=True)
    spring = lax.all_gather(spring_sub, "bead", axis=0, tiled=True)
    return (result[:, 0], result[:, 1], spring)


def solution(mesh):
    return jax.shard_map(
        on_device,
        mesh=mesh,
        in_specs=(
            P("bead", None, "atom"),
            P("bead", None, "atom"),
            P("atom"),
            P("atom"),
            P("atom"),
            P("atom"),
            P("atom"),
        ),
        out_specs=(P("bead", None, "atom"), P("bead", None, "atom"), P("atom")),
        check_vma=False,
    )
```

profile of v0, /device:TPU:0, one launch (start us, length us, event | category | flops | bytes accessed | tf_op | source)
XLA Modules:
  0.0 81.9 jit_solution(6459633473460166946)
XLA Ops:
  0.6 0.7 broadcast_in_dim.86
  1.3 0.8 pad_maximum_fusion.3
  2.2 3.0 %collective-permute-start = (f32[4,4,1024]{2,0,1:T(4,128)S(1)}, f32[4,4,1024]{2,0,1:T(4,128)S(1)}, u32[]{:S(2)}, u32[]{:S(2)}) collective-permute-start(f32[4,4,1024]{2,0,1:T(4,128)S(1)} %pad_maximum_fusion.3), channel_id=1, source_target_pairs={{0,1},{1,2},{2,3},{3,0},{4,5},{5,6},{6,7},{7,4},{8,9},{9,10},{10,1... | collective-permute-start | bytes 196616 | tf_op jit(solution)/shard_map/ppermute | solution.py:17
  5.2 1.0 %collective-permute-start.1 = (f32[4,4,1024]{2,0,1:T(4,128)S(1)}, f32[4,4,1024]{2,0,1:T(4,128)S(1)}, u32[]{:S(2)}, u32[]{:S(2)}) collective-permute-start(f32[4,4,1024]{2,0,1:T(4,128)S(1)} %pad_maximum_fusion.3), channel_id=1, source_target_pairs={{1,0},{2,1},{3,2},{0,3},{5,4},{6,5},{7,6},{4,7},{9,8},{10,9},{11,1... | collective-permute-start | bytes 196616 | tf_op jit(solution)/shard_map/ppermute | solution.py:20
  6.2 1.6 %copy.64 = f32[4,3,1024]{0,1,2:T(4,128)S(1)} copy(f32[4,3,1024]{2,0,1:T(4,128)} %param.11) | data formatting | bytes 98304 | tf_op args[0]
  7.8 1.9 %reshape.224 = f32[8,1,1536]{2,1,0:T(1,128)} reshape(f32[1024,3,4]{2,1,0:T(4,128)S(1)} %bitcast.89) | data formatting | bytes 98304
  9.7 5.3 %all-to-all-start = ((f32[8,1,1536]{2,1,0:T(1,128)}), f32[8,1,1536]{2,1,0:T(1,128)S(1)}, u32[]{:S(2)}, u32[]{:S(2)}) async-start(f32[8,1,1536]{2,1,0:T(1,128)} %reshape.224), calls=%async_computation | async-start | bytes 98304 | tf_op jit(solution)/shard_map/all_to_all | solution.py:99
  16.0 0.8 broadcast_multiply_fusion
  17.2 0.7 gather_fusion
  18.3 0.7 gather_fusion.1
  19.4 27.1 %while.10 = (s32[]{:T(128)}, f32[8,4,4,3,128]{4,3,2,1,0:T(4,128)S(1)}, f32[8,4,2,4,4,128]{5,3,1,4,2,0:T(4,128)S(1)}, s32[]{:T(128)}) while((s32[]{:T(128)}, f32[8,4,4,3,128]{4,3,2,1,0:T(4,128)S(1)}, f32[8,4,2,4,4,128]{5,3,1,4,2,0:T(4,128)S(1)}, s32[]{:T(128)}) %tuple.40), condition=%wide.region_3.5_spmd, body=%wide.region_0.4_spmd.sunk | while | flops 5761026 | bytes 4759613 | solution.py:83
  19.5 1.0 %fusion.62 = f32[4,4,128,128]{3,2,1,0:T(8,128)S(1)} fusion(f32[4,4,3,128]{3,2,1,0:T(4,128)S(1)} %copy.92, f32[4,4,3,128]{3,2,1,0:T(4,128)S(1)} %copy.93), kind=kLoop, calls=%fused_computation.4.clone.1 | loop fusion | flops 2097152 | bytes 1097728 | tf_op jit(solution)/shard_map/while/body/eval_jaxpr/reduce_sum | solution.py:47
  20.9 1.9 %fusion.63 = f32[4,4,3,128]{3,2,1,0:T(4,128)S(1)} fusion(f32[4,4,128,128]{3,2,1,0:T(8,128)S(1)} %multiply_multiply_fusion.5, f32[4,4,3,128]{3,2,1,0:T(4,128)S(1)} %copy.92, f32[4,4,3,128]{3,2,1,0:T(4,128)S(1)} %copy.93), kind=kLoop, calls=%fused_computation.5.clone.1 | loop fusion | flops 2353152 | bytes 1122304 | tf_op jit(solution)/shard_map/while/body/eval_jaxpr/reduce_sum | solution.py:54
  22.9 1.0 %fusion.62 = f32[4,4,128,128]{3,2,1,0:T(8,128)S(1)} fusion(f32[4,4,3,128]{3,2,1,0:T(4,128)S(1)} %copy.92, f32[4,4,3,128]{3,2,1,0:T(4,128)S(1)} %copy.93), kind=kLoop, calls=%fused_computation.4.clone.1 | loop fusion | flops 2097152 | bytes 1097728 | tf_op jit(solution)/shard_map/while/body/eval_jaxpr/reduce_sum | solution.py:47
  24.3 1.9 %fusion.63 = f32[4,4,3,128]{3,2,1,0:T(4,128)S(1)} fusion(f32[4,4,128,128]{3,2,1,0:T(8,128)S(1)} %multiply_multiply_fusion.5, f32[4,4,3,128]{3,2,1,0:T(4,128)S(1)} %copy.92, f32[4,4,3,128]{3,2,1,0:T(4,128)S(1)} %copy.93), kind=kLoop, calls=%fused_computation.5.clone.1 | loop fusion | flops 2353152 | bytes 1122304 | tf_op jit(solution)/shard_map/while/body/eval_jaxpr/reduce_sum | solution.py:54
  26.3 1.0 %fusion.62 = f32[4,4,128,128]{3,2,1,0:T(8,128)S(1)} fusion(f32[4,4,3,128]{3,2,1,0:T(4,128)S(1)} %copy.92, f32[4,4,3,128]{3,2,1,0:T(4,128)S(1)} %copy.93), kind=kLoop, calls=%fused_computation.4.clone.1 | loop fusion | flops 2097152 | bytes 1097728 | tf_op jit(solution)/shard_map/while/body/eval_jaxpr/reduce_sum | solution.py:47
  27.3 0.3 multiply_multiply_fusion.5
  27.7 1.9 %fusion.63 = f32[4,4,3,128]{3,2,1,0:T(4,128)S(1)} fusion(f32[4,4,128,128]{3,2,1,0:T(8,128)S(1)} %multiply_multiply_fusion.5, f32[4,4,3,128]{3,2,1,0:T(4,128)S(1)} %copy.92, f32[4,4,3,128]{3,2,1,0:T(4,128)S(1)} %copy.93), kind=kLoop, calls=%fused_computation.5.clone.1 | loop fusion | flops 2353152 | bytes 1122304 | tf_op jit(solution)/shard_map/while/body/eval_jaxpr/reduce_sum | solution.py:54
  29.7 1.0 %fusion.62 = f32[4,4,128,128]{3,2,1,0:T(8,128)S(1)} fusion(f32[4,4,3,128]{3,2,1,0:T(4,128)S(1)} %copy.92, f32[4,4,3,128]{3,2,1,0:T(4,128)S(1)} %copy.93), kind=kLoop, calls=%fused_computation.4.clone.1 | loop fusion | flops 2097152 | bytes 1097728 | tf_op jit(solution)/shard_map/while/body/eval_jaxpr/reduce_sum | solution.py:47
  31.1 1.9 %fusion.63 = f32[4,4,3,128]{3,2,1,0:T(4,128)S(1)} fusion(f32[4,4,128,128]{3,2,1,0:T(8,128)S(1)} %multiply_multiply_fusion.5, f32[4,4,3,128]{3,2,1,0:T(4,128)S(1)} %copy.92, f32[4,4,3,128]{3,2,1,0:T(4,128)S(1)} %copy.93), kind=kLoop, calls=%fused_computation.5.clone.1 | loop fusion | flops 2353152 | bytes 1122304 | tf_op jit(solution)/shard_map/while/body/eval_jaxpr/reduce_sum | solution.py:54
  33.0 1.0 %fusion.62 = f32[4,4,128,128]{3,2,1,0:T(8,128)S(1)} fusion(f32[4,4,3,128]{3,2,1,0:T(4,128)S(1)} %copy.92, f32[4,4,3,128]{3,2,1,0:T(4,128)S(1)} %copy.93), kind=kLoop, calls=%fused_computation.4.clone.1 | loop fusion | flops 2097152 | bytes 1097728 | tf_op jit(solution)/shard_map/while/body/eval_jaxpr/reduce_sum | solution.py:47
  34.5 1.9 %fusion.63 = f32[4,4,3,128]{3,2,1,0:T(4,128)S(1)} fusion(f32[4,4,128,128]{3,2,1,0:T(8,128)S(1)} %multiply_multiply_fusion.5, f32[4,4,3,128]{3,2,1,0:T(4,128)S(1)} %copy.92, f32[4,4,3,128]{3,2,1,0:T(4,128)S(1)} %copy.93), kind=kLoop, calls=%fused_computation.5.clone.1 | loop fusion | flops 2353152 | bytes 1122304 | tf_op jit(solution)/shard_map/while/body/eval_jaxpr/reduce_sum | solution.py:54
  36.4 1.0 %fusion.62 = f32[4,4,128,128]{3,2,1,0:T(8,128)S(1)} fusion(f32[4,4,3,128]{3,2,1,0:T(4,128)S(1)} %copy.92, f32[4,4,3,128]{3,2,1,0:T(4,128)S(1)} %copy.93), kind=kLoop, calls=%fused_computation.4.clone.1 | loop fusion | flops 2097152 | bytes 1097728 | tf_op jit(solution)/shard_map/while/body/eval_jaxpr/reduce_sum | solution.py:47
  37.5 0.3 multiply_multiply_fusion.5
  37.8 1.9 %fusion.63 = f32[4,4,3,128]{3,2,1,0:T(4,128)S(1)} fusion(f32[4,4,128,128]{3,2,1,0:T(8,128)S(1)} %multiply_multiply_fusion.5, f32[4,4,3,128]{3,2,1,0:T(4,128)S(1)} %copy.92, f32[4,4,3,128]{3,2,1,0:T(4,128)S(1)} %copy.93), kind=kLoop, calls=%fused_computation.5.clone.1 | loop fusion | flops 2353152 | bytes 1122304 | tf_op jit(solution)/shard_map/while/body/eval_jaxpr/reduce_sum | solution.py:54
  39.8 1.0 %fusion.62 = f32[4,4,128,128]{3,2,1,0:T(8,128)S(1)} fusion(f32[4,4,3,128]{3,2,1,0:T(4,128)S(1)} %copy.92, f32[4,4,3,128]{3,2,1,0:T(4,128)S(1)} %copy.93), kind=kLoop, calls=%fused_computation.4.clone.1 | loop fusion | flops 2097152 | bytes 1097728 | tf_op jit(solution)/shard_map/while/body/eval_jaxpr/reduce_sum | solution.py:47
  41.2 1.9 %fusion.63 = f32[4,4,3,128]{3,2,1,0:T(4,128)S(1)} fusion(f32[4,4,128,128]{3,2,1,0:T(8,128)S(1)} %multiply_multiply_fusion.5, f32[4,4,3,128]{3,2,1,0:T(4,128)S(1)} %copy.92, f32[4,4,3,128]{3,2,1,0:T(4,128)S(1)} %copy.93), kind=kLoop, calls=%fused_computation.5.clone.1 | loop fusion | flops 2353152 | bytes 1122304 | tf_op jit(solution)/shard_map/while/body/eval_jaxpr/reduce_sum | solution.py:54
  43.2 1.0 %fusion.62 = f32[4,4,128,128]{3,2,1,0:T(8,128)S(1)} fusion(f32[4,4,3,128]{3,2,1,0:T(4,128)S(1)} %copy.92, f32[4,4,3,128]{3,2,1,0:T(4,128)S(1)} %copy.93), kind=kLoop, calls=%fused_computation.4.clone.1 | loop fusion | flops 2097152 | bytes 1097728 | tf_op jit(solution)/shard_map/while/body/eval_jaxpr/reduce_sum | solution.py:47
  44.6 1.9 %fusion.63 = f32[4,4,3,128]{3,2,1,0:T(4,128)S(1)} fusion(f32[4,4,128,128]{3,2,1,0:T(8,128)S(1)} %multiply_multiply_fusion.5, f32[4,4,3,128]{3,2,1,0:T(4,128)S(1)} %copy.92, f32[4,4,3,128]{3,2,1,0:T(4,128)S(1)} %copy.93), kind=kLoop, calls=%fused_computation.5.clone.1 | loop fusion | flops 2353152 | bytes 1122304 | tf_op jit(solution)/shard_map/while/body/eval_jaxpr/reduce_sum | solution.py:54
  46.8 0.9 %copy.73 = f32[4,3,1024]{0,1,2:T(4,128)S(1)} copy(f32[4,3,1024]{2,0,1:T(4,128)S(1)} %add.36) | data formatting | bytes 98304 | tf_op jit(solution)/shard_map/add | solution.py:119
  47.7 1.9 %reshape.222 = f32[8,1,1536]{2,1,0:T(1,128)} reshape(f32[1024,3,4]{2,1,0:T(4,128)S(1)} %bitcast.86) | data formatting | bytes 98304
  49.6 5.1 %all-to-all-start.1 = ((f32[8,1,1536]{2,1,0:T(1,128)}), f32[8,1,1536]{2,1,0:T(1,128)S(1)}, u32[]{:S(2)}, u32[]{:S(2)}) async-start(f32[8,1,1536]{2,1,0:T(1,128)} %reshape.222), calls=%async_computation.1 | async-start | bytes 98304 | tf_op jit(solution)/shard_map/all_to_all | solution.py:120
  54.7 0.5 broadcast.235
  55.2 0.8 reduce.1
  56.0 1.2 %reshape.225 = f32[1024,3,4]{2,1,0:T(4,128)S(1)} reshape(f32[8,1536]{1,0:T(8,128)S(1)} %reduce.1) | data formatting | bytes 98304
  57.2 0.7 copy.65
  57.9 2.6 %all-to-all-done.1 = f32[8,1,1536]{2,1,0:T(1,128)S(1)} async-done(((f32[8,1,1536]{2,1,0:T(1,128)}), f32[8,1,1536]{2,1,0:T(1,128)S(1)}, u32[]{:S(2)}, u32[]{:S(2)}) %all-to-all-start.1) | async-done | bytes 49184 | tf_op jit(solution)/shard_map/all_to_all | solution.py:120
  60.5 0.8 reduce
  61.3 1.2 %reshape.223 = f32[1024,3,4]{2,1,0:T(4,128)S(1)} reshape(f32[8,1536]{1,0:T(8,128)S(1)} %reduce) | data formatting | bytes 98304
  62.5 0.7 copy.74
  63.2 0.4 fusion.10
  63.6 0.4 fusion.8
  64.0 0.4 fusion.4
  64.4 0.7 copy.76
  65.1 3.4 %all-to-all-start.2 = ((f32[32,2,3,128]{3,1,2,0:T(2,128)}), f32[32,2,3,128]{3,1,2,0:T(2,128)S(1)}, u32[]{:S(2)}, u32[]{:S(2)}) async-start(f32[32,2,3,128]{3,1,2,0:T(2,128)} %copy.76), calls=%async_computation.2 | async-start | bytes 196608 | tf_op jit(solution)/shard_map/all_to_all | solution.py:127
  68.5 12.1 %all-gather = f32[8,1,128]{2,1,0:T(1,128)S(1)} all-gather(f32[1,1,128]{2,1,0:T(1,128)S(1)} %multiply_bitcast_fusion), channel_id=1, replica_groups=mesh['bead'=8,'atom'=4] {'bead'}, dimensions={0}, use_global_device_ids=true | all-gather | bytes 4608 | tf_op jit(solution)/shard_map/all_gather | solution.py:128
  80.7 0.6 slice_bitcast_fusion.4
  81.3 0.6 copy.104
  (98 shorter events, 4.4 us)
Async XLA Ops:
  2.1 12.8 %copy-start.2 = (s32[32]{0:T(128)S(1)}, s32[32]{0:T(128)}, u32[]{:S(2)}) copy-start(s32[32]{0:T(128)} %param.15) | copy-start | bytes 388
  2.1 13.8 %copy-start.3 = (s32[32]{0:T(128)S(1)}, s32[32]{0:T(128)}, u32[]{:S(2)}) copy-start(s32[32]{0:T(128)} %param.16) | copy-start | bytes 388
  2.2 14.7 %copy-start = (f32[4,3,1024]{2,0,1:T(4,128)S(1)}, f32[4,3,1024]{2,0,1:T(4,128)}, u32[]{:S(2)}) copy-start(f32[4,3,1024]{2,0,1:T(4,128)} %param.11) | copy-start | bytes 147460
  2.2 14.7 %collective-permute-start = (f32[4,4,1024]{2,0,1:T(4,128)S(1)}, f32[4,4,1024]{2,0,1:T(4,128)S(1)}, u32[]{:S(2)}, u32[]{:S(2)}) collective-permute-start(f32[4,4,1024]{2,0,1:T(4,128)S(1)} %pad_maximum_fusion.3), channel_id=1, source_target_pairs={{0,1},{1,2},{2,3},{3,0},{4,5},{5,6},{6,7},{7,4},{8,9},{9,10},{10,1... | collective-permute-start | bytes 196616 | tf_op jit(solution)/shard_map/ppermute | solution.py:17
  5.2 11.7 %collective-permute-start.1 = (f32[4,4,1024]{2,0,1:T(4,128)S(1)}, f32[4,4,1024]{2,0,1:T(4,128)S(1)}, u32[]{:S(2)}, u32[]{:S(2)}) collective-permute-start(f32[4,4,1024]{2,0,1:T(4,128)S(1)} %pad_maximum_fusion.3), channel_id=1, source_target_pairs={{1,0},{2,1},{3,2},{0,3},{5,4},{6,5},{7,6},{4,7},{9,8},{10,9},{11,1... | collective-permute-start | bytes 196616 | tf_op jit(solution)/shard_map/ppermute | solution.py:20
  9.7 39.9 %all-to-all-start = ((f32[8,1,1536]{2,1,0:T(1,128)}), f32[8,1,1536]{2,1,0:T(1,128)S(1)}, u32[]{:S(2)}, u32[]{:S(2)}) async-start(f32[8,1,1536]{2,1,0:T(1,128)} %reshape.224), calls=%async_computation | async-start | bytes 98304 | tf_op jit(solution)/shard_map/all_to_all | solution.py:99
  19.4 27.4 %copy-start.1 = (f32[4,3,1024]{2,0,1:T(4,128)S(1)}, f32[4,3,1024]{2,0,1:T(4,128)}, u32[]{:S(2)}) copy-start(f32[4,3,1024]{2,0,1:T(4,128)} %param.12) | copy-start | bytes 147460
  49.6 10.9 %all-to-all-start.1 = ((f32[8,1,1536]{2,1,0:T(1,128)}), f32[8,1,1536]{2,1,0:T(1,128)S(1)}, u32[]{:S(2)}, u32[]{:S(2)}) async-start(f32[8,1,1536]{2,1,0:T(1,128)} %reshape.222), calls=%async_computation.1 | async-start | bytes 98304 | tf_op jit(solution)/shard_map/all_to_all | solution.py:120
  65.1 15.5 %all-to-all-start.2 = ((f32[32,2,3,128]{3,1,2,0:T(2,128)}), f32[32,2,3,128]{3,1,2,0:T(2,128)S(1)}, u32[]{:S(2)}, u32[]{:S(2)}) async-start(f32[32,2,3,128]{3,1,2,0:T(2,128)} %copy.76), calls=%async_computation.2 | async-start | bytes 196608 | tf_op jit(solution)/shard_map/all_to_all | solution.py:127
where the time goes:
time: 82.5 us; the launch traced here: 81.9 us
  other arithmetic  30.1 us (36%)
  starting transfers between devices  17.8 us (22%)
  local copies, waits for them, and re-layouts  15.6 us (19%)
  blocking collectives  12.1 us (15%)
  waiting for transfers between devices  2.63 us (3%)
  between operations  1.65 us (2%)
  matrix products  1.39 us (2%)
    reduce_sum x8, other arithmetic, pair_force(): return jnp.sum(separation * weights[..., None, :, :], axis=-1)  14.9 us
    all_gather x1, blocking collectives, on_device(): spring = lax.all_gather(spring_sub, 'bead', axis=0, tiled=True)  12.1 us
    unnamed x14, local copies, waits for them, and re-layouts  8.41 us
    reduce_sum x8, other arithmetic, pair_force(): dist_sq = jnp.sum(separation * separation, axis=-3)  8.35 us
    all_to_all x1, starting transfers between devices, on_device(): lax.all_to_all(positions, 'bead', split_axis=2, concat_axis=0, tiled=True)  5.29 us
    all_to_all x1, starting transfers between devices, on_device(): lax.all_to_all(kicked, 'bead', split_axis=2, concat_axis=0, tiled=True)  5.09 us
    all_to_all x1, starting transfers between devices, on_device(): lax.all_to_all(returned_rows, 'bead', split_axis=0, concat_axis=3, tiled=...  3.36 us
    ppermute x1, starting transfers between devices, extended(): lax.ppermute(lax.slice_in_dim(block, block.shape[dim] - width, None, axis...  3.02 us
  transfers between devices with their start and end apart: 5, of which 1 were waited for; matrix products, arithmetic and copies ran while one was open for 49% of the time, Pallas kernels for 0%

commit v1 on v0

v1 whole, which is shorter than its diff:
```python
import functools

import jax
import jax.numpy as jnp
import numpy as np
from jax import lax
from jax.experimental import pallas as pl
from jax.experimental.pallas import tpu as pltpu
from jax.sharding import PartitionSpec as P

time_step = 1.0
omega_cycle = 1.2
width_sq = 2.0
LANES = 128
MESH = pl.DeviceIdType.MESH


def step_matrices(beads, bead_dev):
    j = np.arange(beads, dtype=np.float64)[:, None]
    k = np.arange(beads, dtype=np.float64)[None, :]
    middle = beads // 2
    angle = 2.0 * np.pi * ((j * k) % beads) / beads
    table = np.where(k < middle, np.cos(angle), np.sin(angle)) * np.sqrt(2.0 / beads)
    table[:, 0] = np.sqrt(1.0 / beads)
    table[:, middle] = np.sqrt(1.0 / beads) * (1.0 - 2.0 * (np.arange(beads) % 2))
    freq = 2.0 * omega_cycle * np.sin(np.pi * np.arange(beads) / beads)
    cosine, sine = np.cos(freq * time_step), np.sin(freq * time_step)
    reach = np.where(freq > 0, sine / np.where(freq > 0, freq, 1.0), time_step)
    rows = 3 * bead_dev
    groups = 3 * beads // rows
    order = np.arange(3 * beads).reshape(groups, bead_dev, 3).transpose(0, 2, 1).reshape(-1)

    def spread(matrix):
        return np.kron(matrix, np.eye(3))[order][:, order]

    same = spread((table * cosine) @ table.T)
    drift = spread((table * reach) @ table.T)
    pull = spread((table * (freq * sine)) @ table.T)
    bend_pos = spread((freq * cosine)[:, None] * table.T)
    bend_mom = spread((freq * reach)[:, None] * table.T)

    def mixed(top, bottom):
        both = [top.reshape(groups, rows, -1), bottom.reshape(groups, rows, -1)]
        return np.concatenate(both, axis=1).reshape(2 * rows * groups, -1)

    on_pos = np.concatenate([mixed(same, pull), bend_pos])
    on_mom = np.concatenate([mixed(drift, same), bend_mom])
    return np.stack([on_pos, on_mom]).astype(np.float32)


def kernel(
    beads, bead_count, atom_count,
    local_ref, other_ref, count_ref, pos_ref, mom_ref, charge_ref, mass_ref, mat_ref,
    newp_ref, newm_ref, spring_ref,
    halo_pos, halo_charge, rows_own, cols, acc, full, pos_out, pos_in, kick_out, kick_in,
    back_out, back_in, stack_pos, stack_mom,
    halo_send, halo_recv, pos_send, pos_recv, kick_send, kick_recv, back_send, back_recv,
):
    _, bead_dev, atom_dev = pos_ref.shape
    tile_dev = atom_dev // LANES
    slots = local_ref.shape[0]
    sub = atom_dev // bead_count
    rows = 3 * bead_dev
    me = lax.axis_index("bead")
    here = lax.axis_index("atom")
    up = lax.rem(here + 1, atom_count)
    down = lax.rem(here + atom_count - 1, atom_count)

    barrier = pltpu.get_barrier_semaphore()
    for target in (up, down):
        pl.semaphore_signal(barrier, inc=1, device_id={"atom": target}, device_id_type=MESH)
    for o in range(1, bead_count):
        peer = lax.rem(me + o, bead_count)
        pl.semaphore_signal(barrier, inc=1, device_id={"bead": peer}, device_id_type=MESH)

    def split_rows(ref, out):
        for p in range(bead_count):
            for c in range(3):
                r = slice(bead_dev * c, bead_dev * (c + 1))
                out[p, r, :] = ref[c, :, p * sub : (p + 1) * sub]

    split_rows(pos_ref, pos_out)
    pl.semaphore_wait(barrier, bead_count + 1)

    halo = []
    for side, target in ((0, up), (1, down)):
        for which, (src, dst) in enumerate(((pos_ref, halo_pos), (charge_ref, halo_charge))):
            copy = pltpu.make_async_remote_copy(
                src_ref=src, dst_ref=dst.at[side],
                send_sem=halo_send.at[side, which], recv_sem=halo_recv.at[side, which],
                device_id={"atom": target}, device_id_type=MESH,
            )
            copy.start()
            halo.append(copy)

    def exchange(src, dst, send, recv):
        copies = []
        for o in range(1, bead_count):
            peer = lax.rem(me + o, bead_count)
            copy = pltpu.make_async_remote_copy(
                src_ref=src.at[peer], dst_ref=dst.at[me],
                send_sem=send.at[o], recv_sem=recv.at[o],
                device_id={"bead": peer}, device_id_type=MESH,
            )
            copy.start()
            copies.append(copy)
        return copies

    pos_copies = exchange(pos_out, pos_in, pos_send, pos_recv)

    scale = 0.5 * float(np.sqrt(np.log2(np.e)))

    def lay_tile(pos, charge_row, t, slot, own):
        lanes = slice(t * LANES, (t + 1) * LANES)
        parts = [pos[c, :, lanes] * scale for c in range(3)]
        parts.append(charge_row)
        block = jnp.concatenate(parts, axis=0)
        pad = (-block.shape[0]) % 8
        block = jnp.concatenate([block, jnp.zeros((pad, LANES), jnp.float32)], axis=0)
        if own:
            rows_own[t] = block
        cols[slot] = jnp.transpose(block)

    for t in range(tile_dev):
        lay_tile(pos_ref, charge_ref[t : t + 1, :], t, tile_dev + t, True)
    acc[...] = jnp.zeros_like(acc)
    for copy in halo:
        copy.wait_recv()
    for side, first in ((0, 0), (1, 2 * tile_dev)):
        for t in range(tile_dev):
            lay_tile(
                halo_pos.at[side], halo_charge[side, t : t + 1, :], t, first + t, False
            )

    live_count = count_ref[0]
    base = here * tile_dev
    tiles = tile_dev * atom_count

    def slot_step(s, carry):
        left = lax.rem(local_ref[s], tile_dev)
        right = lax.rem(other_ref[s] - base + tile_dev + tiles, tiles)
        right = jnp.minimum(right, 3 * tile_dev - 1)
        block = rows_own[left]
        xa = [jnp.broadcast_to(block[r : r + 1, :], (8, LANES)) for r in range(rows)]
        total = [jnp.zeros((8, LANES), jnp.float32) for _ in range(rows)]
        for i in range(LANES // 8):
            chunk = cols[right, 8 * i : 8 * i + 8, :]
            charge = jnp.broadcast_to(chunk[:, rows : rows + 1], (8, LANES))
            for b in range(bead_dev):
                at = [bead_dev * c + b for c in range(3)]
                d = [
                    xa[r] - jnp.broadcast_to(chunk[:, r : r + 1], (8, LANES)) for r in at
                ]
                weight = charge * jnp.exp2(-(d[0] * d[0] + d[1] * d[1] + d[2] * d[2]))
                for c in range(3):
                    total[at[c]] = total[at[c]] + weight * d[c]
        summed = jnp.concatenate([jnp.sum(v, axis=0, keepdims=True) for v in total], axis=0)
        live = jnp.where(s < live_count, 2.0 / width_sq * 0.5 / scale, 0.0)
        summed = summed * (block[rows : rows + 1, :] * live)
        for t in range(tile_dev):
            acc[t] = acc[t] + summed * jnp.where(left == t, 1.0, 0.0)
        return carry

    lax.fori_loop(0, slots, slot_step, 0)

    for t in range(tile_dev):
        full[:, t * LANES : (t + 1) * LANES] = acc[t]
    for p in range(bead_count):
        mine = slice(p * sub, (p + 1) * sub)
        for c in range(3):
            r = slice(bead_dev * c, bead_dev * (c + 1))
            kick_out[p, r, :] = mom_ref[c, :, mine] + (0.5 * time_step) * full[r, mine]
    kick_copies = exchange(kick_out, kick_in, kick_send, kick_recv)

    pos_in[me] = pos_out[me]
    kick_in[me] = kick_out[me]
    for copy in pos_copies:
        copy.wait_recv()
    for p in range(bead_count):
        stack_pos[p * rows : (p + 1) * rows, :] = pos_in[p]

    def times(m, x):
        return jnp.dot(
            m, x, precision=lax.Precision.HIGHEST, preferred_element_type=jnp.float32
        )

    from_pos = times(mat_ref[0], stack_pos[...])
    mass = mass_ref[pl.ds(me, 1), :]
    inverse = 1.0 / mass
    for copy in kick_copies:
        copy.wait_recv()
    for p in range(bead_count):
        stack_mom[p * rows : (p + 1) * rows, :] = kick_in[p]
    from_mom = times(mat_ref[1], stack_mom[...])
    both = 2 * rows
    is_pos = lax.broadcasted_iota(jnp.int32, (both, sub), 0) < rows
    weight_pos = jnp.where(is_pos, 1.0, -mass)
    weight_mom = jnp.where(is_pos, inverse, 1.0)
    split = both * bead_count
    bend = from_pos[split:] + from_mom[split:] * inverse
    spring = jnp.sum(bend * bend, axis=0, keepdims=True) * (0.5 * mass) * (1.0 / beads)
    for p in range(bead_count):
        r = slice(p * both, (p + 1) * both)
        back_out[p, :both, :] = from_pos[r] * weight_pos + from_mom[r] * weight_mom
        back_out[p, both : both + 1, :] = spring
    back_copies = exchange(back_out, back_in, back_send, back_recv)
    back_in[me] = back_out[me]
    for copy in back_copies:
        copy.wait_recv()
    for p in range(bead_count):
        mine = slice(p * sub, (p + 1) * sub)
        for c in range(3):
            first = bead_dev * c
            newp_ref[c, :, mine] = back_in[p, first : first + bead_dev, :]
            newm_ref[c, :, mine] = back_in[p, rows + first : rows + first + bead_dev, :]
        spring_ref[:, mine] = back_in[p, both : both + 1, :]
    for copy in halo + pos_copies + kick_copies + back_copies:
        copy.wait_send()


def on_device(positions, momenta, charge, masses, pair_local, pair_other, pair_count):
    positions = jnp.transpose(positions, (1, 0, 2))
    momenta = jnp.transpose(momenta, (1, 0, 2))
    _, bead_dev, atom_dev = positions.shape
    bead_count = lax.axis_size("bead")
    atom_count = lax.axis_size("atom")
    beads = bead_dev * bead_count
    tile_dev = atom_dev // LANES
    sub = atom_dev // bead_count
    rows = 3 * bead_dev
    wide = rows + 1 + (-(rows + 1)) % 8
    f32 = jnp.float32
    vmem = pl.BlockSpec(memory_space=pltpu.VMEM)
    smem = pl.BlockSpec(memory_space=pltpu.SMEM)
    dma = pltpu.SemaphoreType.DMA
    new_positions, new_momenta, spring = pl.pallas_call(
        functools.partial(kernel, beads, bead_count, atom_count),
        out_shape=(
            jax.ShapeDtypeStruct(positions.shape, f32),
            jax.ShapeDtypeStruct(positions.shape, f32),
            jax.ShapeDtypeStruct((1, atom_dev), f32),
        ),
        in_specs=[smem] * 3 + [vmem] * 5,
        out_specs=(vmem, vmem, vmem),
        scratch_shapes=[
            pltpu.VMEM((2,) + positions.shape, f32),
            pltpu.VMEM((2, tile_dev, LANES), f32),
            pltpu.VMEM((tile_dev, wide, LANES), f32),
            pltpu.VMEM((3 * tile_dev, LANES, wide), f32),
            pltpu.VMEM((tile_dev, rows, LANES), f32),
            pltpu.VMEM((rows, atom_dev), f32),
            pltpu.VMEM((bead_count, rows, sub), f32),
            pltpu.VMEM((bead_count, rows, sub), f32),
            pltpu.VMEM((bead_count, rows, sub), f32),
            pltpu.VMEM((bead_count, rows, sub), f32),
            pltpu.VMEM((bead_count, 2 * rows + 1, sub), f32),
            pltpu.VMEM((bead_count, 2 * rows + 1, sub), f32),
            pltpu.VMEM((3 * beads, sub), f32),
            pltpu.VMEM((3 * beads, sub), f32),
            dma((2, 2)),
            dma((2, 2)),
        ]
        + [dma((bead_count,))] * 6,
        compiler_params=pltpu.CompilerParams(collective_id=0, has_side_effects=True),
    )(
        pair_local, pair_other, pair_count, positions, momenta,
        charge.reshape(tile_dev, LANES), masses.reshape(bead_count, sub),
        jnp.asarray(step_matrices(beads, bead_dev)),
    )
    back = (1, 0, 2)
    return (
        jnp.transpose(new_positions, back),
        jnp.transpose(new_momenta, back),
        spring.reshape(atom_dev),
    )


def solution(mesh):
    return jax.shard_map(
        on_device,
        mesh=mesh,
        in_specs=(
            P("bead", None, "atom"),
            P("bead", None, "atom"),
            P("atom"),
            P("atom"),
            P("atom"),
            P("atom"),
            P("atom"),
        ),
        out_specs=(P("bead", None, "atom"), P("bead", None, "atom"), P("atom")),
        check_vma=False,
    )
```

time: 82.5 us -> 39.8 us (0.48)
  Pallas kernels: 0 us -> 35.5 us
  other arithmetic: 30.1 us -> 0 us
  starting transfers between devices: 17.8 us -> 0 us
  local copies, waits for them, and re-layouts: 15.6 us -> 2.72 us
  blocking collectives: 12.1 us -> 0 us
  waiting for transfers between devices: 2.63 us -> 0 us
  matrix products: 1.39 us -> 0 us
    pallas_call x0 -> x1, Pallas kernels: none -> 35.5 us  [on_device(): pl.pallas_call(functools.partial(kernel, beads, bead_count, atom_count),...]
    reduce_sum x16 -> x0, other arithmetic: 23.2 us -> none  [the longest x8 14.9 us: pair_force(): return jnp.sum(separation * weights[..., None, :, :], axis=-1)]
    all_to_all x3 -> x0, starting transfers between devices: 13.7 us -> none  [the longest x1 5.29 us: on_device(): lax.all_to_all(positions, 'bead', split_axis=2, concat_axis=0, tiled=True)]
    all_gather x1 -> x0, blocking collectives: 12.1 us -> none  [on_device(): spring = lax.all_gather(spring_sub, 'bead', axis=0, tiled=True)]
    unnamed x14 -> x7, local copies, waits for them, and re-layouts: 8.41 us -> 2.72 us
    ppermute x2 -> x0, starting transfers between devices: 4.04 us -> none  [the longest x1 3.02 us: extended(): lax.ppermute(lax.slice_in_dim(block, block.shape[dim] - width, None, axis...]
    div x8 -> x0, other arithmetic: 2.72 us -> none  [pair_force(): left_charge[..., :, None] * right_charge[..., None, :]]
    all_to_all x3 -> x0, waiting for transfers between devices: 2.62 us -> none  [the longest x1 2.61 us: on_device(): lax.all_to_all(kicked, 'bead', split_axis=2, concat_axis=0, tiled=True)]
  transfers between devices with their start and end apart: 5 -> 0, of which waited for: 1 -> 0; matrix products, arithmetic and copies ran while one was open for 49% -> 0% of each run, Pallas kernels for 0% -> 0%
where the time goes in v1:
time: 39.8 us; the launch traced here: 39.6 us
  Pallas kernels  35.5 us (89%)
  local copies, waits for them, and re-layouts  2.72 us (7%)
  between operations  1.3 us (3%)
    pallas_call x1, Pallas kernels, on_device(): pl.pallas_call(functools.partial(kernel, beads, bead_count, atom_count),...  35.5 us
    unnamed x7, local copies, waits for them, and re-layouts  2.72 us

profile of v1, /device:TPU:0, one launch (start us, length us, event | category | flops | bytes accessed | tf_op | source)
XLA Modules:
  0.0 39.6 jit_solution(9171578602827803153)
XLA Ops:
  1.3 35.5 %shard_map.103 = (f32[3,4,1024]{2,1,0:T(4,128)}, f32[3,4,1024]{2,1,0:T(4,128)}, f32[1,1024]{1,0:T(1,128)}) custom-call(s32[32]{0:T(128)} %local_ref.1, s32[32]{0:T(128)} %other_ref.1, s32[1]{0:T(128)S(6)} %copy.14.count_ref, f32[3,4,1024]{2,1,0:T(4,128)} %bitcast.7, f32[3,4,1024]{2,1,0:T(4,128)} %bitcast.8, f32[8,128]{1,0:T(8,128)} %bitcast.11, ...), custom_call_target="tpu_custom_call" | custom-call | tf_op jit(solution)/shard_map/pallas_call | solution.py:236
  36.8 0.0 copy-start
  36.8 1.4 %copy.15 = f32[4,3,1024]{2,0,1:T(4,128)} copy(f32[4,3,1024]{2,0,1:T(4,128)} %bitcast.10) | data formatting | bytes 98304
  38.3 0.0 copy-done
  38.3 0.0 copy-start.1
  38.3 0.6 %copy.16 = f32[4,3,1024]{2,0,1:T(4,128)} copy(f32[4,3,1024]{2,0,1:T(4,128)S(1)} %bitcast.9) | data formatting | bytes 98304
  38.9 0.1 copy-done.1
  39.0 0.6 %copy.17 = f32[1024]{0:T(1024)} copy(f32[1024]{0:T(1024)S(1)} %bitcast.13) | data formatting | bytes 8192
Async XLA Ops:
  36.8 1.4 %copy-start = (f32[3,4,1024]{2,1,0:T(4,128)S(1)}, f32[3,4,1024]{2,1,0:T(4,128)}, u32[]{:S(2)}) copy-start(f32[3,4,1024]{2,1,0:T(4,128)} %get-tuple-element.7) | copy-start | bytes 147460
  38.3 0.7 %copy-start.1 = (f32[1,1024]{1,0:T(1,128)S(1)}, f32[1,1024]{1,0:T(1,128)}, u32[]{:S(2)}) copy-start(f32[1,1024]{1,0:T(1,128)} %get-tuple-element.8) | copy-start | bytes 12292

commit v2 on v1

--- a/solution.py
+++ b/solution.py
@@ -52,7 +52,7 @@
     beads, bead_count, atom_count,
     local_ref, other_ref, count_ref, pos_ref, mom_ref, charge_ref, mass_ref, mat_ref,
     newp_ref, newm_ref, spring_ref,
-    halo_pos, halo_charge, rows_own, cols, acc, full, pos_out, pos_in, kick_out, kick_in,
+    halo_pos, halo_charge, own, cols, cols_charge, acc, full, pos_out, pos_in, kick_out, kick_in,
     back_out, back_in, stack_pos, stack_mom,
     halo_send, halo_recv, pos_send, pos_recv, kick_send, kick_recv, back_send, back_recv,
 ):
@@ -110,16 +110,30 @@
 
     scale = 0.5 * float(np.sqrt(np.log2(np.e)))
 
-    def lay_tile(pos, charge_row, t, slot, own):
+    blocks = [bead_dev * c + b for b in range(bead_dev) for c in range(3)]
+    tall = rows + (-rows) % 16
+    row = lax.rem(lax.broadcasted_iota(jnp.int32, (3 * tall, LANES), 0), tall)
+    picks = jnp.concatenate([jnp.where(row == r, -1.0, 0.0) for r in blocks], axis=1)
+    picks = picks.astype(jnp.bfloat16)
+
+    def lay_tile(pos, charge_row, t, slot, mine):
         lanes = slice(t * LANES, (t + 1) * LANES)
-        parts = [pos[c, :, lanes] * scale for c in range(3)]
-        parts.append(charge_row)
-        block = jnp.concatenate(parts, axis=0)
-        pad = (-block.shape[0]) % 8
-        block = jnp.concatenate([block, jnp.zeros((pad, LANES), jnp.float32)], axis=0)
-        if own:
-            rows_own[t] = block
-        cols[slot] = jnp.transpose(block)
+        block = jnp.concatenate([pos[c, :, lanes] * scale for c in range(3)], axis=0)
+        parts = []
+        for _ in range(3):
+            part = block.astype(jnp.bfloat16).astype(jnp.float32)
+            block = block - part
+            parts.append(part)
+        pad = jnp.zeros((tall - rows, LANES), jnp.float32)
+        laid = [v for part in parts for v in (part, pad)]
+        laid.append(jnp.ones((tall, LANES), jnp.float32))
+        cols[slot] = jnp.transpose(jnp.concatenate(laid, axis=0)).astype(jnp.bfloat16)
+        cols_charge[slot] = jnp.transpose(jnp.broadcast_to(charge_row, (8, LANES)))
+        if mine:
+            flat = [jnp.concatenate([v[r : r + 1] for r in blocks], axis=1) for v in parts]
+            flat.append(jnp.zeros((tall - 3, len(blocks) * LANES), jnp.float32))
+            own[t, : 3 * tall, :] = picks
+            own[t, 3 * tall :, :] = jnp.concatenate(flat, axis=0).astype(jnp.bfloat16)
 
     for t in range(tile_dev):
         lay_tile(pos_ref, charge_ref[t : t + 1, :], t, tile_dev + t, True)
@@ -140,23 +154,28 @@
         left = lax.rem(local_ref[s], tile_dev)
         right = lax.rem(other_ref[s] - base + tile_dev + tiles, tiles)
         right = jnp.minimum(right, 3 * tile_dev - 1)
-        block = rows_own[left]
-        xa = [jnp.broadcast_to(block[r : r + 1, :], (8, LANES)) for r in range(rows)]
         total = [jnp.zeros((8, LANES), jnp.float32) for _ in range(rows)]
-        for i in range(LANES // 8):
-            chunk = cols[right, 8 * i : 8 * i + 8, :]
-            charge = jnp.broadcast_to(chunk[:, rows : rows + 1], (8, LANES))
-            for b in range(bead_dev):
-                at = [bead_dev * c + b for c in range(3)]
-                d = [
-                    xa[r] - jnp.broadcast_to(chunk[:, r : r + 1], (8, LANES)) for r in at
-                ]
-                weight = charge * jnp.exp2(-(d[0] * d[0] + d[1] * d[1] + d[2] * d[2]))
-                for c in range(3):
-                    total[at[c]] = total[at[c]] + weight * d[c]
+        together = 2
+        for first in range(0, bead_dev, together):
+            wide = slice(3 * first * LANES, 3 * (first + together) * LANES)
+            apart = jnp.dot(
+                cols[right], own[left, :, wide], preferred_element_type=jnp.float32
+            )
+            for i in range(LANES // 8):
+                e = slice(8 * i, 8 * i + 8)
+                charge = jnp.broadcast_to(cols_charge[right, e, 0:1], (8, LANES))
+                for b in range(together):
+                    n = [3 * b + c for c in range(3)]
+                    d = [apart[e, m * LANES : (m + 1) * LANES] for m in n]
+                    weight = charge * jnp.exp2(
+                        -(d[0] * d[0] + d[1] * d[1] + d[2] * d[2])
+                    )
+                    for c in range(3):
+                        r = bead_dev * c + first + b
+                        total[r] = total[r] + weight * d[c]
         summed = jnp.concatenate([jnp.sum(v, axis=0, keepdims=True) for v in total], axis=0)
         live = jnp.where(s < live_count, 2.0 / width_sq * 0.5 / scale, 0.0)
-        summed = summed * (block[rows : rows + 1, :] * live)
+        summed = summed * (charge_ref[pl.ds(left, 1), :] * live)
         for t in range(tile_dev):
             acc[t] = acc[t] + summed * jnp.where(left == t, 1.0, 0.0)
         return carry
@@ -228,7 +247,7 @@
     tile_dev = atom_dev // LANES
     sub = atom_dev // bead_count
     rows = 3 * bead_dev
-    wide = rows + 1 + (-(rows + 1)) % 8
+    deep = 4 * (rows + (-rows) % 16)
     f32 = jnp.float32
     vmem = pl.BlockSpec(memory_space=pltpu.VMEM)
     smem = pl.BlockSpec(memory_space=pltpu.SMEM)
@@ -245,8 +264,9 @@
         scratch_shapes=[
             pltpu.VMEM((2,) + positions.shape, f32),
             pltpu.VMEM((2, tile_dev, LANES), f32),
-            pltpu.VMEM((tile_dev, wide, LANES), f32),
-            pltpu.VMEM((3 * tile_dev, LANES, wide), f32),
+            pltpu.VMEM((tile_dev, deep, rows * LANES), jnp.bfloat16),
+            pltpu.VMEM((3 * tile_dev, LANES, deep), jnp.bfloat16),
+            pltpu.VMEM((3 * tile_dev, LANES, 8), f32),
             pltpu.VMEM((tile_dev, rows, LANES), f32),
             pltpu.VMEM((rows, atom_dev), f32),
             pltpu.VMEM((bead_count, rows, sub), f32),

time: 39.8 us -> 34.6 us (0.87)
  Pallas kernels: 35.5 us -> 30.4 us
    pallas_call x1, Pallas kernels: 35.5 us -> 30.4 us  [on_device(): pl.pallas_call(functools.partial(kernel, beads, bead_count, atom_count),...]
where the time goes in v2:
time: 34.6 us; the launch traced here: 34.4 us
  Pallas kernels  30.4 us (88%)
  local copies, waits for them, and re-layouts  2.72 us (8%)
  between operations  1.3 us (4%)
    pallas_call x1, Pallas kernels, on_device(): pl.pallas_call(functools.partial(kernel, beads, bead_count, atom_count),...  30.4 us
    unnamed x7, local copies, waits for them, and re-layouts  2.72 us

profile of v2, /device:TPU:0, one launch (start us, length us, event | category | flops | bytes accessed | tf_op | source)
XLA Modules:
  0.0 34.4 jit_solution(11057386401918122460)
XLA Ops:
  1.3 30.4 %shard_map.103 = (f32[3,4,1024]{2,1,0:T(4,128)}, f32[3,4,1024]{2,1,0:T(4,128)}, f32[1,1024]{1,0:T(1,128)}) custom-call(s32[32]{0:T(128)} %local_ref.1, s32[32]{0:T(128)} %other_ref.1, s32[1]{0:T(128)S(6)} %copy.14.count_ref, f32[3,4,1024]{2,1,0:T(4,128)} %bitcast.7, f32[3,4,1024]{2,1,0:T(4,128)} %bitcast.8, f32[8,128]{1,0:T(8,128)} %bitcast.11, ...), custom_call_target="tpu_custom_call" | custom-call | tf_op jit(solution)/shard_map/pallas_call | solution.py:255
  31.7 0.0 copy-start
  31.7 1.4 %copy.15 = f32[4,3,1024]{2,0,1:T(4,128)} copy(f32[4,3,1024]{2,0,1:T(4,128)} %bitcast.10) | data formatting | bytes 98304
  33.1 0.0 copy-done
  33.1 0.0 copy-start.1
  33.1 0.6 %copy.16 = f32[4,3,1024]{2,0,1:T(4,128)} copy(f32[4,3,1024]{2,0,1:T(4,128)S(1)} %bitcast.9) | data formatting | bytes 98304
  33.7 0.1 copy-done.1
  33.8 0.6 %copy.17 = f32[1024]{0:T(1024)} copy(f32[1024]{0:T(1024)S(1)} %bitcast.13) | data formatting | bytes 8192
Async XLA Ops:
  31.7 1.4 %copy-start = (f32[3,4,1024]{2,1,0:T(4,128)S(1)}, f32[3,4,1024]{2,1,0:T(4,128)}, u32[]{:S(2)}) copy-start(f32[3,4,1024]{2,1,0:T(4,128)} %get-tuple-element.7) | copy-start | bytes 147460
  33.1 0.7 %copy-start.1 = (f32[1,1024]{1,0:T(1,128)S(1)}, f32[1,1024]{1,0:T(1,128)}, u32[]{:S(2)}) copy-start(f32[1,1024]{1,0:T(1,128)} %get-tuple-element.8) | copy-start | bytes 12292

commit v3 on v2

--- a/solution.py
+++ b/solution.py
@@ -50,8 +50,9 @@
 
 def kernel(
     beads, bead_count, atom_count,
-    local_ref, other_ref, count_ref, pos_ref, mom_ref, charge_ref, mass_ref, mat_ref,
+    local_in, other_in, count_ref, pos_given, mom_given, charge_given, mass_given, mat_given,
     newp_ref, newm_ref, spring_ref,
+    local_ref, other_ref, pos_ref, mom_ref, charge_ref, mass_ref, mat_ref, load_sem,
     halo_pos, halo_charge, own, cols, cols_charge, acc, full, pos_out, pos_in, kick_out, kick_in,
     back_out, back_in, stack_pos, stack_mom,
     halo_send, halo_recv, pos_send, pos_recv, kick_send, kick_recv, back_send, back_recv,
@@ -73,13 +74,26 @@
         peer = lax.rem(me + o, bead_count)
         pl.semaphore_signal(barrier, inc=1, device_id={"bead": peer}, device_id_type=MESH)
 
+    given = (
+        (pos_given, pos_ref), (charge_given, charge_ref), (local_in, local_ref),
+        (other_in, other_ref), (mom_given, mom_ref),
+        (mass_given, mass_ref), (mat_given, mat_ref),
+    )
+    loads = [
+        pltpu.make_async_copy(src, dst, load_sem.at[i]) for i, (src, dst) in enumerate(given)
+    ]
+    for load in loads:
+        load.start()
+
     def split_rows(ref, out):
         for p in range(bead_count):
             for c in range(3):
                 r = slice(bead_dev * c, bead_dev * (c + 1))
                 out[p, r, :] = ref[c, :, p * sub : (p + 1) * sub]
 
+    loads[0].wait()
     split_rows(pos_ref, pos_out)
+    loads[1].wait()
     pl.semaphore_wait(barrier, bead_count + 1)
 
     halo = []
@@ -146,11 +160,13 @@
                 halo_pos.at[side], halo_charge[side, t : t + 1, :], t, first + t, False
             )
 
+    for load in loads[2:]:
+        load.wait()
     live_count = count_ref[0]
     base = here * tile_dev
     tiles = tile_dev * atom_count
 
-    def slot_step(s, carry):
+    def slot_step(s):
         left = lax.rem(local_ref[s], tile_dev)
         right = lax.rem(other_ref[s] - base + tile_dev + tiles, tiles)
         right = jnp.minimum(right, 3 * tile_dev - 1)
@@ -176,11 +192,20 @@
         summed = jnp.concatenate([jnp.sum(v, axis=0, keepdims=True) for v in total], axis=0)
         live = jnp.where(s < live_count, 2.0 / width_sq * 0.5 / scale, 0.0)
         summed = summed * (charge_ref[pl.ds(left, 1), :] * live)
+        return left, summed
+
+    together_slots = 2 if slots % 2 == 0 else 1
+
+    def slots_step(i, carry):
+        done = [slot_step(i * together_slots + k) for k in range(together_slots)]
         for t in range(tile_dev):
-            acc[t] = acc[t] + summed * jnp.where(left == t, 1.0, 0.0)
+            new = acc[t]
+            for left, summed in done:
+                new = new + summed * jnp.where(left == t, 1.0, 0.0)
+            acc[t] = new
         return carry
 
-    lax.fori_loop(0, slots, slot_step, 0)
+    lax.fori_loop(0, slots // together_slots, slots_step, 0)
 
     for t in range(tile_dev):
         full[:, t * LANES : (t + 1) * LANES] = acc[t]
@@ -249,8 +274,9 @@
     rows = 3 * bead_dev
     deep = 4 * (rows + (-rows) % 16)
     f32 = jnp.float32
+    hbm = pl.BlockSpec(memory_space=pl.ANY)
     vmem = pl.BlockSpec(memory_space=pltpu.VMEM)
-    smem = pl.BlockSpec(memory_space=pltpu.SMEM)
+    matrices = step_matrices(beads, bead_dev)
     dma = pltpu.SemaphoreType.DMA
     new_positions, new_momenta, spring = pl.pallas_call(
         functools.partial(kernel, beads, bead_count, atom_count),
@@ -259,9 +285,17 @@
             jax.ShapeDtypeStruct(positions.shape, f32),
             jax.ShapeDtypeStruct((1, atom_dev), f32),
         ),
-        in_specs=[smem] * 3 + [vmem] * 5,
+        in_specs=[hbm, hbm, pl.BlockSpec(memory_space=pltpu.SMEM)] + [hbm] * 5,
         out_specs=(vmem, vmem, vmem),
         scratch_shapes=[
+            pltpu.SMEM(pair_local.shape, jnp.int32),
+            pltpu.SMEM(pair_other.shape, jnp.int32),
+            pltpu.VMEM(positions.shape, f32),
+            pltpu.VMEM(positions.shape, f32),
+            pltpu.VMEM((tile_dev, LANES), f32),
+            pltpu.VMEM((bead_count, sub), f32),
+            pltpu.VMEM(matrices.shape, f32),
+            dma((7,)),
             pltpu.VMEM((2,) + positions.shape, f32),
             pltpu.VMEM((2, tile_dev, LANES), f32),
             pltpu.VMEM((tile_dev, deep, rows * LANES), jnp.bfloat16),
@@ -285,7 +319,7 @@
     )(
         pair_local, pair_other, pair_count, positions, momenta,
         charge.reshape(tile_dev, LANES), masses.reshape(bead_count, sub),
-        jnp.asarray(step_matrices(beads, bead_dev)),
+        jnp.asarray(matrices),
     )
     back = (1, 0, 2)
     return (

time: 34.6 us -> 31.2 us (0.902)
  Pallas kernels: 30.4 us -> 26.9 us
    pallas_call x1, Pallas kernels: 30.4 us -> 26.9 us  [on_device(): pl.pallas_call(functools.partial(kernel, beads, bead_count, atom_count),...]
where the time goes in v3:
time: 31.2 us; the launch traced here: 30.9 us
  Pallas kernels  26.9 us (86%)
  local copies, waits for them, and re-layouts  2.72 us (9%)
  between operations  1.3 us (4%)
    pallas_call x1, Pallas kernels, on_device(): pl.pallas_call(functools.partial(kernel, beads, bead_count, atom_count),...  26.9 us
    unnamed x7, local copies, waits for them, and re-layouts  2.72 us

profile of v3, /device:TPU:0, one launch (start us, length us, event | category | flops | bytes accessed | tf_op | source)
XLA Modules:
  0.0 30.9 jit_solution(4849126241445325306)
XLA Ops:
  1.3 26.9 %shard_map.103 = (f32[3,4,1024]{2,1,0:T(4,128)}, f32[3,4,1024]{2,1,0:T(4,128)}, f32[1,1024]{1,0:T(1,128)}) custom-call(s32[32]{0:T(128)} %local_in.1, s32[32]{0:T(128)} %other_in.1, s32[1]{0:T(128)S(6)} %copy.14.count_ref, f32[3,4,1024]{2,1,0:T(4,128)} %bitcast.7, f32[3,4,1024]{2,1,0:T(4,128)} %bitcast.8, f32[8,128]{1,0:T(8,128)} %bitcast.11, ...), custom_call_target="tpu_custom_call" | custom-call | tf_op jit(solution)/shard_map/pallas_call | solution.py:281
  28.2 0.0 copy-start
  28.2 1.4 %copy.15 = f32[4,3,1024]{2,0,1:T(4,128)} copy(f32[4,3,1024]{2,0,1:T(4,128)} %bitcast.10) | data formatting | bytes 98304
  29.6 0.0 copy-done
  29.6 0.0 copy-start.1
  29.6 0.6 %copy.16 = f32[4,3,1024]{2,0,1:T(4,128)} copy(f32[4,3,1024]{2,0,1:T(4,128)S(1)} %bitcast.9) | data formatting | bytes 98304
  30.3 0.1 copy-done.1
  30.3 0.6 %copy.17 = f32[1024]{0:T(1024)} copy(f32[1024]{0:T(1024)S(1)} %bitcast.13) | data formatting | bytes 8192
Async XLA Ops:
  28.2 1.4 %copy-start = (f32[3,4,1024]{2,1,0:T(4,128)S(1)}, f32[3,4,1024]{2,1,0:T(4,128)}, u32[]{:S(2)}) copy-start(f32[3,4,1024]{2,1,0:T(4,128)} %get-tuple-element.7) | copy-start | bytes 147460
  29.6 0.7 %copy-start.1 = (f32[1,1024]{1,0:T(1,128)S(1)}, f32[1,1024]{1,0:T(1,128)}, u32[]{:S(2)}) copy-start(f32[1,1024]{1,0:T(1,128)} %get-tuple-element.8) | copy-start | bytes 12292

commit v4 on v3

--- a/solution.py
+++ b/solution.py
@@ -260,6 +260,12 @@
         spring_ref[:, mine] = back_in[p, both : both + 1, :]
     for copy in halo + pos_copies + kick_copies + back_copies:
         copy.wait_send()
+
+
+def hand_over(*refs):
+    half = len(refs) // 2
+    for src, dst in zip(refs[:half], refs[half:]):
+        dst[...] = src[...]
 
 
 def on_device(positions, momenta, charge, masses, pair_local, pair_other, pair_count):
@@ -321,6 +327,13 @@
         charge.reshape(tile_dev, LANES), masses.reshape(bead_count, sub),
         jnp.asarray(matrices),
     )
+    results = (new_positions, new_momenta, spring)
+    new_positions, new_momenta, spring = pl.pallas_call(
+        hand_over,
+        out_shape=tuple(jax.ShapeDtypeStruct(v.shape, f32) for v in results),
+        in_specs=[vmem] * 3,
+        out_specs=(vmem,) * 3,
+    )(*results)
     back = (1, 0, 2)
     return (
         jnp.transpose(new_positions, back),

time: 31.2 us -> 29.9 us (0.958)
  local copies, waits for them, and re-layouts: 2.72 us -> 0 us
  Pallas kernels: 26.9 us -> 28.4 us
    unnamed x7 -> x0, local copies, waits for them, and re-layouts: 2.72 us -> none
    pallas_call x0 -> x1, Pallas kernels: none -> 1.47 us  [on_device(): pl.pallas_call(hand_over, out_shape=tuple((jax.ShapeDtypeStruct(v.shape,...]
where the time goes in v4:
time: 29.9 us; the launch traced here: 29.7 us
  Pallas kernels  28.4 us (95%)
  between operations  1.29 us (4%)
    pallas_call x1, Pallas kernels, on_device(): pl.pallas_call(functools.partial(kernel, beads, bead_count, atom_count),...  26.9 us
    pallas_call x1, Pallas kernels, on_device(): pl.pallas_call(hand_over, out_shape=tuple((jax.ShapeDtypeStruct(v.shape,...  1.47 us

profile of v4, /device:TPU:0, one launch (start us, length us, event | category | flops | bytes accessed | tf_op | source)
XLA Modules:
  0.0 29.7 jit_solution(11585236335701121960)
XLA Ops:
  1.3 26.9 %shard_map.103 = (f32[3,4,1024]{2,1,0:T(4,128)}, f32[3,4,1024]{2,1,0:T(4,128)}, f32[1,1024]{1,0:T(1,128)}) custom-call(s32[32]{0:T(128)} %local_in.1, s32[32]{0:T(128)} %other_in.1, s32[1]{0:T(128)S(6)} %copy.11.count_ref, f32[3,4,1024]{2,1,0:T(4,128)} %bitcast.7, f32[3,4,1024]{2,1,0:T(4,128)} %bitcast.8, f32[8,128]{1,0:T(8,128)} %bitcast.9, ...), custom_call_target="tpu_custom_call" | custom-call | tf_op jit(solution)/shard_map/pallas_call | solution.py:287
  28.2 1.5 %shard_map.104 = (f32[3,4,1024]{2,1,0:T(4,128)}, f32[3,4,1024]{2,1,0:T(4,128)}, f32[1,1024]{1,0:T(1,128)}) custom-call(f32[3,4,1024]{2,1,0:T(4,128)} %get-tuple-element.9.refs_0_, f32[3,4,1024]{2,1,0:T(4,128)} %get-tuple-element.10.refs_1_, f32[1,1024]{1,0:T(1,128)} %get-tuple-element.11.refs_2_), custom_call_target="tpu_custom_call" | custom-call | tf_op jit(solution)/shard_map/pallas_call | solution.py:331

commit v5 on v4

--- a/solution.py
+++ b/solution.py
@@ -194,7 +194,7 @@
         summed = summed * (charge_ref[pl.ds(left, 1), :] * live)
         return left, summed
 
-    together_slots = 2 if slots % 2 == 0 else 1
+    together_slots = 4 if slots % 4 == 0 else 1
 
     def slots_step(i, carry):
         done = [slot_step(i * together_slots + k) for k in range(together_slots)]

time: 29.9 us -> 28.9 us (0.967)
  Pallas kernels: 28.4 us -> 27.4 us
    pallas_call x1, Pallas kernels: 26.9 us -> 25.9 us  [on_device(): pl.pallas_call(functools.partial(kernel, beads, bead_count, atom_count),...]
where the time goes in v5:
time: 28.9 us; the launch traced here: 28.7 us
  Pallas kernels  27.4 us (95%)
  between operations  1.29 us (4%)
    pallas_call x1, Pallas kernels, on_device(): pl.pallas_call(functools.partial(kernel, beads, bead_count, atom_count),...  25.9 us
    pallas_call x1, Pallas kernels, on_device(): pl.pallas_call(hand_over, out_shape=tuple((jax.ShapeDtypeStruct(v.shape,...  1.47 us

profile of v5, /device:TPU:0, one launch (start us, length us, event | category | flops | bytes accessed | tf_op | source)
XLA Modules:
  0.0 28.7 jit_solution(2477756362442601257)
XLA Ops:
  1.3 25.9 %shard_map.103 = (f32[3,4,1024]{2,1,0:T(4,128)}, f32[3,4,1024]{2,1,0:T(4,128)}, f32[1,1024]{1,0:T(1,128)}) custom-call(s32[32]{0:T(128)} %local_in.1, s32[32]{0:T(128)} %other_in.1, s32[1]{0:T(128)S(6)} %copy.11.count_ref, f32[3,4,1024]{2,1,0:T(4,128)} %bitcast.7, f32[3,4,1024]{2,1,0:T(4,128)} %bitcast.8, f32[8,128]{1,0:T(8,128)} %bitcast.9, ...), custom_call_target="tpu_custom_call" | custom-call | tf_op jit(solution)/shard_map/pallas_call | solution.py:287
  27.2 1.5 %shard_map.104 = (f32[3,4,1024]{2,1,0:T(4,128)}, f32[3,4,1024]{2,1,0:T(4,128)}, f32[1,1024]{1,0:T(1,128)}) custom-call(f32[3,4,1024]{2,1,0:T(4,128)} %get-tuple-element.9.refs_0_, f32[3,4,1024]{2,1,0:T(4,128)} %get-tuple-element.10.refs_1_, f32[1,1024]{1,0:T(1,128)} %get-tuple-element.11.refs_2_), custom_call_target="tpu_custom_call" | custom-call | tf_op jit(solution)/shard_map/pallas_call | solution.py:331
